TPU v7x, 32 devices: a whole 2x2x4 slice. The times are simulated.
32 devices in a mesh: ctx: 16 (over z, x, core), tp: 2 (over y).
Axes of the slice: x: 2, y: 2, z: 4, core: 2. Of those that a mesh axis runs over, the one named last changes fastest.
Arguments:
- queries: bfloat16 [32, 3, 128, 128], P('ctx', None, 'tp'), may hold values from -480 to 480
- prefix_keys: bfloat16 [32768, 8, 128], P('ctx', 'tp'), may hold values from -6 to 6
- prefix_values: bfloat16 [32768, 8, 128], P('ctx', 'tp'), may hold values from -6 to 6
- suffix_keys: bfloat16 [32, 512, 8, 128], P('ctx', None, 'tp'), may hold values from -6 to 6
- suffix_values: bfloat16 [32, 512, 8, 128], P('ctx', None, 'tp'), may hold values from -6 to 6
- fork_lengths: int32 [32], P('ctx'), may hold values from 1 to 509, 8192 in all
- out_weight: bfloat16 [16384, 16384], P('tp', 'ctx'), may hold values from -0.046875 to 0.046875
Outputs:
- projected: bfloat16 [32, 3, 16384], P('tp', None, 'ctx')
Inputs may be any that keep to these rules, and one draw needn't show every extreme that they name: `fork_lengths`: A fork's earlier tokens fill the first slots of its suffix, followed by the keys and values of its 3 new tokens.
All inputs are finite; a program needn't handle non-finite values. No bound on the sum of `fork_lengths` on one device may be relied on, other than what follows from the above.
Results may differ from a plain program's by a relative error of at most 0.014.
Values may be sent and summed in bfloat16 or wider, within the bound.
A program may use at most 128 MiB of HBM per device.

v0:
```python
import math

import jax
import jax.numpy as jnp
from jax import lax
from jax.sharding import PartitionSpec as P


def combine(first, second):
    mixed_a, highest_a, totals_a = first
    mixed_b, highest_b, totals_b = second
    summit = jnp.maximum(highest_a, highest_b)
    factor_a = jnp.exp(highest_a - summit)
    factor_b = jnp.exp(highest_b - summit)
    mixed = mixed_a * factor_a[..., None] + mixed_b * factor_b[..., None]
    return (mixed, summit, totals_a * factor_a + totals_b * factor_b)


def softmax_state(scores, values, form, shape):
    highest = jnp.max(scores, axis=-1)
    weights = jnp.exp(scores - highest[..., None])
    totals = jnp.sum(weights, axis=-1)
    mixed = jnp.einsum(
        form, weights.astype(jnp.bfloat16), values, preferred_element_type=jnp.float32
    )
    return (mixed.reshape(shape), highest.reshape(shape[:3]), totals.reshape(shape[:3]))


def shards(
    queries, prefix_keys, prefix_values, suffix_keys, suffix_values, fork_lengths, out_weight
):
    own_forks, steps, heads_local, head_size = queries.shape
    kv_local = prefix_keys.shape[1]
    group = heads_local // kv_local
    slots = suffix_keys.shape[1]
    scale = head_size ** (-0.5)
    every_query = lax.all_gather(queries, "ctx", axis=0, tiled=True)
    all_forks = every_query.shape[0]
    width = math.gcd(all_forks, 16)
    blocks = all_forks // width

    def prefix_block(block_queries):
        grouped = block_queries.reshape(width, steps, kv_local, group, head_size)
        scores = (
            jnp.einsum("bskgd,pkd->bskgp", grouped, prefix_keys, preferred_element_type=jnp.float32)
            * scale
        )
        return softmax_state(scores, prefix_values, "bskgp,pkd->bskgd", block_queries.shape)

    stacked = lax.map(
        prefix_block, every_query.reshape(blocks, width, steps, heads_local, head_size)
    )
    prefix_state = (
        stacked[0].reshape(all_forks, steps, heads_local, head_size),
        stacked[1].reshape(all_forks, steps, heads_local),
        stacked[2].reshape(all_forks, steps, heads_local),
    )
    grouped = queries.reshape(own_forks, steps, kv_local, group, head_size)
    scores = (
        jnp.einsum("bskgd,bpkd->bskgp", grouped, suffix_keys, preferred_element_type=jnp.float32)
        * scale
    )
    limit = fork_lengths[:, None] + jnp.arange(steps, dtype=jnp.int32)[None, :] + 1
    visible = jnp.arange(slots, dtype=jnp.int32)[None, None, :] < limit[:, :, None]
    scores = jnp.where(visible[:, :, None, None, :], scores, jnp.float32(-1e30))
    own_state = softmax_state(scores, suffix_values, "bskgp,bpkd->bskgd", queries.shape)
    received = lax.all_to_all(
        tuple((piece[None] for piece in prefix_state)),
        "ctx",
        split_axis=1,
        concat_axis=0,
        tiled=True,
    )
    summit = jnp.max(received[1], axis=0)
    factors = jnp.exp(received[1] - summit[None])
    gathered_mixed = jnp.sum(received[0] * factors[..., None], axis=0)
    gathered_totals = jnp.sum(received[2] * factors, axis=0)
    mixed, highest, totals = combine((gathered_mixed, summit, gathered_totals), own_state)
    own_attention = (
        (mixed / totals[..., None])
        .astype(jnp.bfloat16)
        .reshape(own_forks, steps, heads_local * head_size)
    )
    attention = lax.all_gather(own_attention, "ctx", axis=0, tiled=True)
    product = jnp.dot(
        attention.reshape(
            all_forks // lax.axis_size("tp") * lax.axis_size("tp") * steps, heads_local * head_size
        ),
        out_weight,
        preferred_element_type=jnp.float32,
    )
    return lax.psum_scatter(
        product.reshape(
            all_forks // lax.axis_size("tp") * lax.axis_size("tp"), steps, out_weight.shape[1]
        ).astype(jnp.bfloat16),
        "tp",
        scatter_dimension=0,
        tiled=True,
    )


def solution(mesh):
    return jax.shard_map(
        shards,
        mesh=mesh,
        in_specs=(
            P("ctx", None, "tp", None),
            P("ctx", "tp", None),
            P("ctx", "tp", None),
            P("ctx", None, "tp", None),
            P("ctx", None, "tp", None),
            P("ctx"),
            P("tp", "ctx"),
        ),
        out_specs=P("tp", None, "ctx"),
        check_vma=False,
    )
```

profile of v0, /device:TPU:0, one launch (start us, length us, event | category | flops | bytes accessed | tf_op | source)
XLA Modules:
  0.0 289.9 jit_solution(11958791074303953425)
XLA Ops:
  6.5 0.7 all-gather.3.cloned.1.call-update
  7.3 2.0 copy.108
  9.5 1.7 copy.109
  11.2 40.8 %all-gather.3.cloned.1.call-done = bf16[32,3,64,128]{3,2,1,0:T(8,128)(2,1)} async-done(((bf16[2,3,64,128]{3,2,1,0:T(8,128)(2,1)}), bf16[32,3,64,128]{3,2,1,0:T(8,128)(2,1)}) %all-gather.3.cloned.1.call-update) | async-done | bytes 1572880 | tf_op jit(solution)/shard_map/all_gather | solution.py:37
  52.0 69.8 %while.14 = (s32[]{:T(128)}, f32[2,16,3,64,128]{4,3,2,1,0:T(8,128)}, f32[2,16,3,64]{3,1,0,2:T(8,128)S(1)}, f32[2,16,3,64]{3,1,0,2:T(8,128)S(1)}, bf16[2,16,3,64,...) while((s32[]{:T(128)}, ...), condition=%wide.region_3.4_spmd, body=%wide.region_0.3_spmd.sunk | while | flops 3271550976 | bytes 90161752 | solution.py:50
  52.0 1.2 constant_dynamic-slice_fusion.2
  53.2 10.1 %bitcast_reduce_fusion.2 = (f32[16,3,4,16]{3,1,0,2:T(4,128)S(1)}, f32[4,16,3,16,2048]{4,3,2,1,0:T(8,128)}) fusion(bf16[2048,4,128]{2,0,1:T(8,128)(2,1)S(1)} %get-tuple-element.193, bf16[16,3,4,16,128]{4,3,2,1,0:T(8,128)(2,1)S(1)} %bitcast.103), kind=kOutput, calls=%fused_computation.1.clone.1 | convolution fusion | flops 1623192576 | bytes 28061696 | tf_op jit(solution)/shard_map/while/body/eval_jaxpr/bskgd,pkd->bskgp/dot_general | solution.py:45
  63.2 10.8 %fusion.46 = f32[16,3,4,16]{3,1,0,2:T(4,128)S(1)} fusion(f32[4,16,3,16,2048]{4,3,2,1,0:T(8,128)} %get-tuple-element.168, f32[16,3,4,16]{3,1,0,2:T(4,128)S(1)} %get-tuple-element.169), kind=kLoop, calls=%fused_computation.3.clone.1 | loop fusion | flops 18871296 | bytes 25190400 | tf_op jit(solution)/shard_map/while/body/eval_jaxpr/reduce_sum | solution.py:22
  74.5 10.8 %fusion.45 = f32[16,3,4,16,128]{4,3,1,0,2:T(8,128)S(1)} fusion(bf16[2048,4,128]{2,0,1:T(8,128)(2,1)} %get-tuple-element.194, f32[4,16,3,16,2048]{4,3,2,1,0:T(8,128)} %get-tuple-element.168, f32[16,3,4,16]{3,1,0,2:T(4,128)S(1)} %get-tuple-element.169), kind=kOutput, calls=%fused_computation.9.clone.1 | convolution fusion | flops 1629487104 | bytes 28848128 | tf_op jit(solution)/shard_map/while/body/eval_jaxpr/bskgp,pkd->bskgd/dot_general | solution.py:23
  85.6 1.3 constant_dynamic-update-slice_fusion.2
  86.9 1.2 constant_dynamic-slice_fusion.2
  88.1 10.1 %bitcast_reduce_fusion.2 = (f32[16,3,4,16]{3,1,0,2:T(4,128)S(1)}, f32[4,16,3,16,2048]{4,3,2,1,0:T(8,128)}) fusion(bf16[2048,4,128]{2,0,1:T(8,128)(2,1)S(1)} %get-tuple-element.193, bf16[16,3,4,16,128]{4,3,2,1,0:T(8,128)(2,1)S(1)} %bitcast.103), kind=kOutput, calls=%fused_computation.1.clone.1 | convolution fusion | flops 1623192576 | bytes 28061696 | tf_op jit(solution)/shard_map/while/body/eval_jaxpr/bskgd,pkd->bskgp/dot_general | solution.py:45
  98.2 10.8 %fusion.46 = f32[16,3,4,16]{3,1,0,2:T(4,128)S(1)} fusion(f32[4,16,3,16,2048]{4,3,2,1,0:T(8,128)} %get-tuple-element.168, f32[16,3,4,16]{3,1,0,2:T(4,128)S(1)} %get-tuple-element.169), kind=kLoop, calls=%fused_computation.3.clone.1 | loop fusion | flops 18871296 | bytes 25190400 | tf_op jit(solution)/shard_map/while/body/eval_jaxpr/reduce_sum | solution.py:22
  109.4 10.8 %fusion.45 = f32[16,3,4,16,128]{4,3,1,0,2:T(8,128)S(1)} fusion(bf16[2048,4,128]{2,0,1:T(8,128)(2,1)} %get-tuple-element.194, f32[4,16,3,16,2048]{4,3,2,1,0:T(8,128)} %get-tuple-element.168, f32[16,3,4,16]{3,1,0,2:T(4,128)S(1)} %get-tuple-element.169), kind=kOutput, calls=%fused_computation.9.clone.1 | convolution fusion | flops 1629487104 | bytes 28848128 | tf_op jit(solution)/shard_map/while/body/eval_jaxpr/bskgp,pkd->bskgd/dot_general | solution.py:23
  120.5 1.3 constant_dynamic-update-slice_fusion.2
  121.8 0.5 broadcast.64
  122.3 0.7 reduce.2
  123.0 0.7 reshape.132
  123.7 3.5 %all-to-all-start.1 = ((f32[16,1,384]{2,1,0:T(1,128)}), f32[16,1,384]{2,1,0:T(1,128)S(1)}, u32[]{:S(2)}, u32[]{:S(2)}) async-start(f32[16,1,384]{2,1,0:T(1,128)} %reshape.132), calls=%async_computation.1 | async-start | bytes 49152 | tf_op jit(solution)/shard_map/all_to_all | solution.py:67
  127.2 0.7 reduce
  128.0 5.7 %all-to-all-done.1 = f32[16,1,384]{2,1,0:T(1,128)S(1)} async-done(((f32[16,1,384]{2,1,0:T(1,128)}), f32[16,1,384]{2,1,0:T(1,128)S(1)}, u32[]{:S(2)}, u32[]{:S(2)}) %all-to-all-start.1) | async-done | bytes 24608 | tf_op jit(solution)/shard_map/all_to_all | solution.py:67
  133.7 9.1 %all_to_all.36 = f32[16,1,384]{2,1,0:T(1,128)S(1)} all-to-all(f32[16,1,384]{2,1,0:T(1,128)S(1)} %reshape.134), channel_id=1, replica_groups=mesh['ctx'=16,'tp'=2] {'ctx'}, dimensions={0} | all-to-all | bytes 49152 | tf_op jit(solution)/shard_map/all_to_all | solution.py:67
  142.8 4.6 %all-to-all-start = ((f32[1,32,3,64,128]{4,3,2,0,1:T(8,128)}), f32[1,32,3,64,128]{4,3,2,0,1:T(8,128)}, u32[]{:S(2)}, u32[]{:S(2)}) async-start(f32[1,32,3,64,128]{4,3,2,0,1:T(8,128)} %bitcast.9), calls=%async_computation | async-start | bytes 6291456 | tf_op jit(solution)/shard_map/all_to_all | solution.py:67
  147.7 0.6 fusion.38
  149.3 0.6 reduce.3
  150.0 0.6 reduce.1
  151.3 55.3 %all-to-all-done = f32[1,32,3,64,128]{4,3,2,0,1:T(8,128)} async-done(((f32[1,32,3,64,128]{4,3,2,0,1:T(8,128)}), f32[1,32,3,64,128]{4,3,2,0,1:T(8,128)}, u32[]{:S(2)}, u32[]{:S(2)}) %all-to-all-start) | async-done | bytes 3145760 | tf_op jit(solution)/shard_map/all_to_all | solution.py:67
  206.7 2.4 multiply_reduce_fusion
  209.5 0.7 copy.132
  210.5 52.1 %all-gather.5.cloned.1.call-done = bf16[32,3,8192]{2,1,0:T(4,128)(2,1)} async-done(((bf16[2,3,8192]{2,1,0:T(4,128)(2,1)}), bf16[32,3,8192]{2,1,0:T(4,128)(2,1)}) %all-gather.5.cloned.1.call-update) | async-done | bytes 1572880 | tf_op jit(solution)/shard_map/all_gather | solution.py:84
  262.6 10.8 %fusion.20 = bf16[32,3,1024]{2,0,1:T(8,128)(2,1)} fusion(bf16[8192,1024]{1,0:T(8,128)(2,1)} %param.15, bf16[32,3,8192]{2,1,0:T(4,128)(2,1)} %all-gather.5.cloned.1.call-done), kind=kOutput, calls=%fused_computation.23 | convolution fusion | flops 1610711040 | bytes 18546688 | tf_op jit(solution)/shard_map/dot_general | solution.py:85
  273.5 9.9 %reduce-scatter.2.cloned.1.call-done = bf16[16,3,1024]{2,0,1:T(8,128)(2,1)} async-done(((bf16[32,3,1024]{2,0,1:T(8,128)(2,1)}), bf16[16,3,1024]{2,0,1:T(8,128)(2,1)}) %reduce-scatter.2.cloned.1.call-update) | async-done | bytes 98320 | tf_op jit(solution)/shard_map/reduce_scatter | solution.py:92
  (61 shorter events, 4.2 us)
Async XLA Ops:
  6.5 142.2 %copy-start = (bf16[2,512,4,128]{3,2,1,0:T(4,128)(2,1)S(1)}, bf16[2,512,4,128]{3,2,1,0:T(4,128)(2,1)}, u32[]{:S(2)}) copy-start(bf16[2,512,4,128]{3,2,1,0:T(4,128)(2,1)} %param.13) | copy-start | bytes 3145732
  6.5 45.4 %all-gather.3.cloned.1.call-start = ((), (), s32[]{:S(2)}) async-start(), calls=%async_computation.4 | async-start | bytes 1671168 | tf_op jit(solution)/shard_map/all_gather | solution.py:37
  7.3 2.2 copy-start.1
  123.7 10.0 %all-to-all-start.1 = ((f32[16,1,384]{2,1,0:T(1,128)}), f32[16,1,384]{2,1,0:T(1,128)S(1)}, u32[]{:S(2)}, u32[]{:S(2)}) async-start(f32[16,1,384]{2,1,0:T(1,128)} %reshape.132), calls=%async_computation.1 | async-start | bytes 49152 | tf_op jit(solution)/shard_map/all_to_all | solution.py:67
  142.8 4.7 %copy-start.4 = (s32[2]{0:T(128)S(1)}, s32[2]{0:T(128)}, u32[]{:S(2)}) copy-start(s32[2]{0:T(128)} %param.14) | copy-start | bytes 28
  142.8 4.8 %copy-start.2 = (bf16[2,3,64,128]{3,2,1,0:T(8,128)(2,1)S(1)}, bf16[2,3,64,128]{3,2,1,0:T(8,128)(2,1)}, u32[]{:S(2)}) copy-start(bf16[2,3,64,128]{3,2,1,0:T(8,128)(2,1)} %param.9) | copy-start | bytes 294916
  142.8 4.8 %copy-start.3 = (bf16[2,512,4,128]{3,2,1,0:T(4,128)(2,1)S(1)}, bf16[2,512,4,128]{3,2,1,0:T(4,128)(2,1)}, u32[]{:S(2)}) copy-start(bf16[2,512,4,128]{3,2,1,0:T(4,128)(2,1)} %param.12) | copy-start | bytes 3145732
  142.8 63.8 %all-to-all-start = ((f32[1,32,3,64,128]{4,3,2,0,1:T(8,128)}), f32[1,32,3,64,128]{4,3,2,0,1:T(8,128)}, u32[]{:S(2)}, u32[]{:S(2)}) async-start(f32[1,32,3,64,128]{4,3,2,0,1:T(8,128)} %bitcast.9), calls=%async_computation | async-start | bytes 6291456 | tf_op jit(solution)/shard_map/all_to_all | solution.py:67
  147.5 115.2 %all-gather.5.cloned.1.call-start = ((), (), s32[]{:S(2)}) async-start(), calls=%async_computation.5 | async-start | bytes 2228224 | tf_op jit(solution)/shard_map/all_gather | solution.py:84
  210.3 73.1 %reduce-scatter.2.cloned.1.call-start = ((), (), s32[]{:S(2)}) async-start(), calls=%async_computation.6 | async-start | bytes 294912 | tf_op jit(solution)/shard_map/reduce_scatter | solution.py:92
Sparse Core Ops, SparseCore 0:
  9.6 42.3 all-gather.2
  210.4 52.1 all-gather.4
  273.6 9.7 reduce-scatter.1
where the time goes:
time: 290 us
  waiting for transfers between devices  165 us (57%)
  matrix products  53.6 us (18%)
  other arithmetic  27.5 us (9%)
  between operations  13.4 us (5%)
  local copies, waits for them, and re-layouts  13.3 us (5%)
  blocking collectives  9.13 us (3%)
  starting transfers between devices  8.37 us (3%)
    all_to_all x2, waiting for transfers between devices, shards(): lax.all_to_all(tuple((piece[None] for piece in prefix_state)), 'ctx', spl...  61 us
    all_gather x1, waiting for transfers between devices, shards(): attention = lax.all_gather(own_attention, 'ctx', axis=0, tiled=True)  52.1 us
    all_gather x1, waiting for transfers between devices, shards(): every_query = lax.all_gather(queries, 'ctx', axis=0, tiled=True)  40.8 us
    dot_general x3, matrix products, softmax_state(): jnp.einsum(form, weights.astype(jnp.bfloat16), values, preferred_element_...  22 us
    reduce_sum x3, other arithmetic, softmax_state(): totals = jnp.sum(weights, axis=-1)  22 us
    dot_general x2, matrix products, prefix_block(): jnp.einsum('bskgd,pkd->bskgp', grouped, prefix_keys, preferred_element_ty...  20.2 us
    dot_general x1, matrix products, shards(): jnp.dot(attention.reshape(all_forks // lax.axis_size('tp') * lax.axis_siz...  10.8 us
    reduce_scatter x1, waiting for transfers between devices, shards(): lax.psum_scatter(product.reshape(all_forks // lax.axis_size('tp') * lax.a...  9.91 us
  transfers between devices with their start and end apart: 5, of which 5 were waited for; matrix products, arithmetic and copies ran while one was open for 3% of the time, Pallas kernels for 0%

commit v1 on v0

v1 whole, which is shorter than its diff:
```python
import functools
import math

import jax
import jax.numpy as jnp
from jax import lax
from jax.experimental import pallas as pl
from jax.experimental.pallas import tpu as pltpu
from jax.sharding import PartitionSpec as P

MESH = pl.DeviceIdType.MESH
F32 = jnp.float32
BF16 = jnp.bfloat16


def attend(
    n,
    steps,
    lengths_ref,
    q_ref,
    k_ref,
    v_ref,
    sk_ref,
    sv_ref,
    out_ref,
    q_all,
    own,
    own_st,
    psend,
    psend_st,
    precv,
    precv_st,
    csend,
    csend_st,
    crecv,
    crecv_st,
    suf,
    suf_st,
    att,
    qs_sem,
    qr_sem,
    ps_sem,
    pr_sem,
    pss_sem,
    prs_sem,
    cs_sem,
    cr_sem,
    css_sem,
    crs_sem,
    as_sem,
    ar_sem,
):
    kv, rows, hd = q_ref.shape
    forks = sk_ref.shape[0]
    slots = sk_ref.shape[2]
    group = rows // (forks * steps)
    chips = n // 2
    factor = hd ** (-0.5) * math.log2(math.e)
    me = lax.axis_index("ctx")

    def across(mask):
        place, bit = me, 1
        while bit <= mask:
            if mask & bit:
                place = place + bit - 2 * bit * (me // bit % 2)
            bit = 2 * bit
        return place

    barrier = pltpu.get_barrier_semaphore()
    peers = [1] + [2 * chip for chip in range(1, chips)]
    for peer in peers:
        pl.semaphore_signal(
            barrier, inc=1, device_id={"ctx": across(peer)}, device_id_type=MESH
        )
    pl.semaphore_wait(barrier, len(peers))

    def send(source, target, send_sem, recv_sem, peer):
        copy = pltpu.make_async_remote_copy(
            src_ref=source,
            dst_ref=target,
            send_sem=send_sem,
            recv_sem=recv_sem,
            device_id={"ctx": across(peer)},
            device_id_type=MESH,
        )
        copy.start()
        return copy

    class Gather:
        def __init__(self, buf, own_block, send_sems, recv_sems):
            self.buf, self.own_block = buf, own_block
            self.send_sems, self.recv_sems = send_sems, recv_sems
            self.copies = []

        def push(self, slot, peer):
            source = self.own_block if slot == 0 else self.buf.at[slot]
            self.copies.append(
                send(
                    source,
                    self.buf.at[slot ^ peer],
                    self.send_sems.at[len(self.copies)],
                    self.recv_sems.at[slot ^ peer],
                    peer,
                )
            )

        def arrive(self, slot):
            pltpu.make_async_remote_copy(
                src_ref=self.own_block,
                dst_ref=self.buf.at[slot],
                send_sem=self.send_sems.at[0],
                recv_sem=self.recv_sems.at[slot],
                device_id={"ctx": across(1)},
                device_id_type=MESH,
            ).wait_recv()

        def begin(self):
            for chip in range(chips - 2, 0, -2):
                self.push(0, 2 * chip)
            if chips > 1:
                self.push(0, 2)
            self.push(0, 1)

        def near(self):
            self.arrive(2)
            self.push(2, 1)
            self.arrive(1)
            self.arrive(3)

        def far(self):
            for chip in range(2, chips, 2):
                self.arrive(2 * chip)
                self.push(2 * chip, 2)
                self.push(2 * chip, 1)
            for chip in range(3, chips, 2):
                self.arrive(2 * chip)
                self.push(2 * chip, 1)
            for chip in range(2, chips):
                self.arrive(2 * chip + 1)

        def finish(self):
            for copy in self.copies:
                copy.wait_send()

    queries = Gather(q_all, q_ref, qs_sem, qr_sem)
    queries.begin()
    diagonal = lax.broadcasted_iota(jnp.int32, (rows, hd), 0) == lax.broadcasted_iota(
        jnp.int32, (rows, hd), 1
    )

    def to_lanes(column):
        return jnp.sum(
            jnp.where(diagonal, jnp.broadcast_to(column, (rows, hd)), 0.0), axis=0, keepdims=True
        )

    def to_column(lanes):
        return jnp.sum(
            jnp.where(diagonal, jnp.broadcast_to(lanes, (rows, hd)), 0.0), axis=1, keepdims=True
        )

    def state(q, keys, values, visible=None):
        scores = lax.dot_general(
            q, keys, (((1,), (1,)), ((), ())), preferred_element_type=F32
        )
        if visible is not None:
            scores = jnp.where(visible, scores, -1e30)
        highest = jnp.max(scores, axis=1, keepdims=True)
        weights = jnp.exp2((scores - highest) * factor).astype(BF16)
        both = jnp.dot(
            weights,
            jnp.concatenate([values, jnp.ones_like(values)], axis=1),
            preferred_element_type=F32,
        )
        return both[:, :hd], highest * factor, both[:, hd:]

    part = steps * group
    where = lax.broadcasted_iota(jnp.int32, (part, slots), 0) // group
    position = lax.broadcasted_iota(jnp.int32, (part, slots), 1)

    def suffix(head, carry):
        highs, sums = [], []
        for fork in range(forks):
            visible = position < where + (lengths_ref[fork] + 1)
            mixed, high, total = state(
                q_ref[head, pl.ds(fork * part, part), :],
                sk_ref[fork, head],
                sv_ref[fork, head],
                visible,
            )
            suf[head, pl.ds(fork * part, part), :] = mixed
            highs.append(jnp.broadcast_to(high, (part, hd)))
            sums.append(total)
        suf_st[head, 0] = jnp.concatenate(highs, axis=0)
        suf_st[head, 1] = jnp.concatenate(sums, axis=0)
        return carry

    lax.fori_loop(0, kv, suffix, 0)

    def prefix(unit):
        chip = 2 * unit
        places = [2 * chip, 2 * chip + 2, 2 * chip + 1, 2 * chip + 3]

        def one(head, carry):
            q = jnp.concatenate(
                [q_ref[head] if place == 0 else q_all[place, head] for place in places], axis=0
            )
            mixed, high, total = state(q, k_ref[head], v_ref[head])
            for i in range(4):
                block = slice(i * rows, (i + 1) * rows)
                stats, wide = (own_st, own) if i < 2 else (psend_st, psend)
                wide[unit, i % 2, head] = mixed[block].astype(wide.dtype)
                stats[unit, i % 2, pl.ds(2 * head, 1), :] = to_lanes(high[block])
                stats[unit, i % 2, pl.ds(2 * head + 1, 1), :] = to_lanes(total[block])
            return carry

        lax.fori_loop(0, kv, one, 0)
        return (
            send(psend.at[unit], precv.at[unit], ps_sem.at[unit], pr_sem.at[unit], 1),
            send(
                psend_st.at[unit], precv_st.at[unit], pss_sem.at[unit], prs_sem.at[unit], 1
            ),
        )

    outgoing = []

    def pair(unit, copies):
        for copy in copies:
            copy.wait()
        for i in range(2):
            chip = 2 * unit + i
            wide, stats = (csend, csend_st) if chip else (crecv, crecv_st)

            def one(head, carry):
                high_a = own_st[unit, i, pl.ds(2 * head, 1), :]
                high_b = precv_st[unit, i, pl.ds(2 * head, 1), :]
                top = jnp.maximum(high_a, high_b)
                scale_a, scale_b = jnp.exp2(high_a - top), jnp.exp2(high_b - top)
                stats[chip, pl.ds(2 * head, 1), :] = top
                stats[chip, pl.ds(2 * head + 1, 1), :] = (
                    scale_a * own_st[unit, i, pl.ds(2 * head + 1, 1), :]
                    + scale_b * precv_st[unit, i, pl.ds(2 * head + 1, 1), :]
                )
                wide[chip, head] = (
                    own[unit, i, head] * to_column(scale_a)
                    + precv[unit, i, head].astype(F32) * to_column(scale_b)
                ).astype(BF16)
                return carry

            lax.fori_loop(0, kv, one, 0)
            if chip:
                outgoing.append(
                    send(csend.at[chip], crecv.at[chip], cs_sem.at[chip], cr_sem.at[chip], 2 * chip)
                )
                outgoing.append(
                    send(
                        csend_st.at[chip],
                        crecv_st.at[chip],
                        css_sem.at[chip],
                        crs_sem.at[chip],
                        2 * chip,
                    )
                )

    queries.near()
    waiting = (0, prefix(0))
    queries.far()
    for unit in range(chips // 2 - 1, 0, -1):
        copies = prefix(unit)
        pair(*waiting)
        waiting = (unit, copies)
    pair(*waiting)
    queries.finish()
    for copy in outgoing:
        copy.wait()

    def merge(head, carry):
        highs = [crecv_st[chip, pl.ds(2 * head, 1), :] for chip in range(chips)]
        top = functools.reduce(jnp.maximum, highs)
        mixed = jnp.zeros((rows, hd), F32)
        total = jnp.zeros((1, hd), F32)
        for chip in range(chips):
            scale = jnp.exp2(highs[chip] - top)
            total = total + scale * crecv_st[chip, pl.ds(2 * head + 1, 1), :]
            mixed = mixed + crecv[chip, head].astype(F32) * to_column(scale)
        top = to_column(top)
        summit = jnp.maximum(top, suf_st[head, 0])
        scale_a, scale_b = jnp.exp2(top - summit), jnp.exp2(suf_st[head, 0] - summit)
        mixed = mixed * scale_a + suf[head] * scale_b
        total = to_column(total) * scale_a + suf_st[head, 1] * scale_b
        att[0, head] = (mixed / total).astype(BF16)
        return carry

    lax.fori_loop(0, kv, merge, 0)
    attention = Gather(att, att.at[0], as_sem, ar_sem)
    attention.begin()
    attention.near()
    attention.far()
    attention.finish()
    for slot in range(n):
        out_ref[across(slot)] = att[slot]


def shards(
    queries, prefix_keys, prefix_values, suffix_keys, suffix_values, fork_lengths, out_weight
):
    n, tp = lax.axis_size("ctx"), lax.axis_size("tp")
    forks, steps, heads, hd = queries.shape
    kv = prefix_keys.shape[1]
    group = heads // kv
    rows = forks * steps * group
    chips = n // 2
    units = chips // 2
    q = queries.reshape(forks * steps, kv, group, hd).swapaxes(0, 1).reshape(kv, rows, hd)
    vmem = pl.BlockSpec(memory_space=pltpu.VMEM)
    block = (kv, rows, hd)
    stat = (max(8, 2 * kv), hd)
    dma = pltpu.SemaphoreType.DMA
    gathered = pl.pallas_call(
        functools.partial(attend, n, steps),
        out_shape=jax.ShapeDtypeStruct((n,) + block, BF16),
        in_specs=[pl.BlockSpec(memory_space=pltpu.SMEM)] + [vmem] * 5,
        out_specs=vmem,
        scratch_shapes=[
            pltpu.VMEM((n,) + block, BF16),
            pltpu.VMEM((units, 2) + block, F32),
            pltpu.VMEM((units, 2) + stat, F32),
            pltpu.VMEM((units, 2) + block, BF16),
            pltpu.VMEM((units, 2) + stat, F32),
            pltpu.VMEM((units, 2) + block, BF16),
            pltpu.VMEM((units, 2) + stat, F32),
            pltpu.VMEM((chips,) + block, BF16),
            pltpu.VMEM((chips,) + stat, F32),
            pltpu.VMEM((chips,) + block, BF16),
            pltpu.VMEM((chips,) + stat, F32),
            pltpu.VMEM(block, F32),
            pltpu.VMEM((kv, 2, rows, hd), F32),
            pltpu.VMEM((n,) + block, BF16),
            dma((n,)),
            dma((n,)),
            dma((units,)),
            dma((units,)),
            dma((units,)),
            dma((units,)),
            dma((chips,)),
            dma((chips,)),
            dma((chips,)),
            dma((chips,)),
            dma((n,)),
            dma((n,)),
        ],
        compiler_params=pltpu.CompilerParams(
            collective_id=0, has_side_effects=True, vmem_limit_bytes=60 * 1024 * 1024
        ),
    )(
        fork_lengths,
        q,
        prefix_keys.swapaxes(0, 1),
        prefix_values.swapaxes(0, 1),
        suffix_keys.swapaxes(1, 2),
        suffix_values.swapaxes(1, 2),
    )
    attention = (
        gathered.reshape(n, kv, forks * steps, group, hd)
        .transpose(0, 2, 1, 3, 4)
        .reshape(n * forks * steps, heads * hd)
    )
    product = jnp.dot(attention, out_weight, preferred_element_type=F32)
    product = product.reshape(tp, n * forks // tp, steps, -1).astype(BF16)
    mine = lax.axis_index("tp")
    total = lax.dynamic_index_in_dim(product, mine, 0, keepdims=False).astype(F32)
    for shift in range(1, tp):
        piece = lax.dynamic_index_in_dim(product, (mine + shift) % tp, 0, keepdims=False)
        total = total + lax.ppermute(
            piece, "tp", [(i, (i + shift) % tp) for i in range(tp)]
        ).astype(F32)
    return total.astype(BF16)


def solution(mesh):
    return jax.shard_map(
        shards,
        mesh=mesh,
        in_specs=(
            P("ctx", None, "tp", None),
            P("ctx", "tp", None),
            P("ctx", "tp", None),
            P("ctx", None, "tp", None),
            P("ctx", None, "tp", None),
            P("ctx"),
            P("tp", "ctx"),
        ),
        out_specs=P("tp", None, "ctx"),
        check_vma=False,
    )
```

time: 290 us -> 115 us (0.40)
  waiting for transfers between devices: 165 us -> 3.58 us
  Pallas kernels: 0 us -> 84.2 us
  matrix products: 53.6 us -> 9.27 us
  other arithmetic: 27.5 us -> 0.66 us
  between operations: 13.4 us -> 0.04 us
  blocking collectives: 9.13 us -> 0 us
  starting transfers between devices: 8.37 us -> 1.56 us
    all_gather x2 -> x0, waiting for transfers between devices: 92.9 us -> none  [the longest x1 52.1 us: shards(): attention = lax.all_gather(own_attention, 'ctx', axis=0, tiled=True)]
    pallas_call x0 -> x1, Pallas kernels: none -> 84.2 us  [shards(): pl.pallas_call(functools.partial(attend, n, steps), out_shape=jax.ShapeDt...]
    all_to_all x2 -> x0, waiting for transfers between devices: 61 us -> none  [shards(): lax.all_to_all(tuple((piece[None] for piece in prefix_state)), 'ctx', spl...]
    dot_general x7 -> x1, matrix products: 53.6 us -> 9.27 us  [shards(): product = jnp.dot(attention, out_weight, preferred_element_type=F32)]
    reduce_sum x5 -> x0, other arithmetic: 24.4 us -> none  [the longest x3 22 us: softmax_state(): totals = jnp.sum(weights, axis=-1)]
    reduce_scatter x1 -> x0, waiting for transfers between devices: 9.91 us -> none  [shards(): lax.psum_scatter(product.reshape(all_forks // lax.axis_size('tp') * lax.a...]
    all_to_all x1 -> x0, blocking collectives: 9.13 us -> none  [shards(): lax.all_to_all(tuple((piece[None] for piece in prefix_state)), 'ctx', spl...]
    all_to_all x2 -> x0, starting transfers between devices: 8.11 us -> none  [shards(): lax.all_to_all(tuple((piece[None] for piece in prefix_state)), 'ctx', spl...]
  transfers between devices with their start and end apart: 5 -> 1, of which waited for: 5 -> 1; matrix products, arithmetic and copies ran while one was open for 3% -> 0% of each run, Pallas kernels for 0% -> 0%
where the time goes in v1:
time: 115 us; the launch traced here: 114 us
  Pallas kernels  84.2 us (73%)
  local copies, waits for them, and re-layouts  15.1 us (13%)
  matrix products  9.27 us (8%)
  waiting for transfers between devices  3.58 us (3%)
  starting transfers between devices  1.56 us (1%)
    pallas_call x1, Pallas kernels, shards(): pl.pallas_call(functools.partial(attend, n, steps), out_shape=jax.ShapeDt...  84.2 us
    dot_general x1, matrix products, shards(): product = jnp.dot(attention, out_weight, preferred_element_type=F32)  9.27 us
    transpose x1, local copies, waits for them, and re-layouts, shards(): prefix_values.swapaxes(0, 1)  4.85 us
    dot_general x1, local copies, waits for them, and re-layouts, shards(): product = jnp.dot(attention, out_weight, preferred_element_type=F32)  3.97 us
    ppermute x1, waiting for transfers between devices, shards(): lax.ppermute(piece, 'tp', [(i, (i + shift) % tp) for i in range(tp)])  3.58 us
    reshape x1, local copies, waits for them, and re-layouts, shards(): gathered.reshape(n, kv, forks * steps, group, hd).transpose(0, 2, 1, 3, 4)  3.01 us
  transfers between devices with their start and end apart: 1, of which 1 were waited for; matrix products, arithmetic and copies ran while one was open for 0% of the time, Pallas kernels for 0%

profile of v1, /device:TPU:0, one launch (start us, length us, event | category | flops | bytes accessed | tf_op | source)
XLA Modules:
  0.0 114.4 jit_solution(14021258784897997998)
XLA Ops:
  0.0 1.5 %copy.13 = bf16[6,4,16,128]{3,2,0,1:T(8,128)(2,1)} copy(bf16[6,4,16,128]{3,2,1,0:T(8,128)(2,1)} %bitcast.33) | data formatting | bytes 196608 | tf_op jit(solution)/shard_map/reshape | solution.py:313
  1.5 0.0 copy-start
  1.5 0.0 copy-start.1
  1.5 4.8 %copy_bitcast_fusion = (bf16[4,2048,128]{2,1,0:T(8,128)(2,1)}, bf16[4,2048,128]{2,1,0:T(8,128)(2,1)}) fusion(bf16[2048,4,128]{2,1,0:T(4,128)(2,1)} %param.9, bf16[2048,4,128]{2,1,0:T(4,128)(2,1)} %param.8), kind=kLoop, calls=%fused_computation.2 | loop fusion | bytes 8388608 | tf_op jit(solution)/shard_map/transpose | solution.py:358
  6.4 0.0 copy-done
  6.4 0.0 copy-done.1
  6.4 1.7 %copy_bitcast_fusion.3 = (bf16[2,4,512,128]{3,2,1,0:T(8,128)(2,1)}, bf16[2,4,512,128]{3,2,1,0:T(8,128)(2,1)}) fusion(bf16[2,512,4,128]{3,2,1,0:T(4,128)(2,1)S(1)} %copy-done, bf16[2,512,4,128]{3,2,1,0:T(4,128)(2,1)S(1)} %copy-done.1), kind=kLoop, calls=%fused_computation.7 | loop fusion | bytes 4194304 | tf_op jit(solution)/shard_map/transpose | solution.py:360
  8.1 84.2 %shard_map.73 = bf16[16,4,96,128]{3,2,1,0:T(8,128)(2,1)} custom-call(s32[2]{0:T(128)} %lengths_ref.1, bf16[4,96,128]{2,1,0:T(8,128)(2,1)} %bitcast.32, bf16[4,2048,128]{2,1,0:T(8,128)(2,1)} %get-tuple-element.6.k_ref, bf16[4,2048,128]{2,1,0:T(8,128)(2,1)} %get-tuple-element.5.v_ref, bf16[2,4,512,128]{3,2,1,0:T(8,128)(2,1)} %get-tuple-element.8.sk_ref, ...), custom_call_target="tpu_custom_call" | custom-call | tf_op jit(solution)/shard_map/pallas_call | solution.py:318
  92.3 3.0 %copy.30 = bf16[16,4,6,16,128]{4,3,1,2,0:T(8,128)(2,1)} copy(bf16[16,4,6,16,128]{4,3,2,1,0:T(8,128)(2,1)} %bitcast.31) | data formatting | bytes 3145728 | tf_op jit(solution)/shard_map/reshape | solution.py:363
  95.3 4.0 %dot_general.5 = bf16[2,16,3,8192]{3,2,1,0:T(4,128)(2,1)S(1)} reshape(bf16[16,6,4,16,128]{4,3,2,1,0:T(8,128)(2,1)} %bitcast.30) | data formatting | bytes 3145728 | tf_op jit(solution)/shard_map/dot_general | solution.py:367
  99.3 9.3 %fusion.3 = bf16[2,16,3,1024]{3,1,2,0:T(8,128)(2,1)S(1)} fusion(bf16[8192,1024]{1,0:T(8,128)(2,1)} %param.13, bf16[2,16,3,8192]{3,2,1,0:T(4,128)(2,1)S(1)} %dot_general.5), kind=kOutput, calls=%fused_computation.6 | convolution fusion | flops 1610711040 | bytes 18546688 | tf_op jit(solution)/shard_map/dot_general | solution.py:367
  108.6 1.6 %collective-permute-start = (bf16[16,3,1024]{2,0,1:T(8,128)(2,1)S(1)}, bf16[16,3,1024]{2,0,1:T(8,128)(2,1)S(1)}, u32[]{:S(2)}, u32[]{:S(2)}) collective-permute-start(bf16[16,3,1024]{2,0,1:T(8,128)(2,1)S(1)} %dynamic-slice_bitcast_fusion), channel_id=1, source_target_pairs={{0,1},{1,0},{2,3},{3,2},{4,5},{5,4},{6,7},{7,6},{8,9},{9,8},{10,11... | collective-permute-start | bytes 294920 | tf_op jit(solution)/shard_map/ppermute | solution.py:373
  110.2 3.6 %collective-permute-done = bf16[16,3,1024]{2,0,1:T(8,128)(2,1)S(1)} collective-permute-done((bf16[16,3,1024]{2,0,1:T(8,128)(2,1)S(1)}, bf16[16,3,1024]{2,0,1:T(8,128)(2,1)S(1)}, u32[]{:S(2)}, u32[]{:S(2)}) %collective-permute-start) | collective-permute-done | bytes 98336 | tf_op jit(solution)/shard_map/ppermute | solution.py:373
  113.8 0.7 fusion.8
  (1 shorter events, 0.0 us)
Async XLA Ops:
  1.5 4.9 %copy-start = (bf16[2,512,4,128]{3,2,1,0:T(4,128)(2,1)S(1)}, bf16[2,512,4,128]{3,2,1,0:T(4,128)(2,1)}, u32[]{:S(2)}) copy-start(bf16[2,512,4,128]{3,2,1,0:T(4,128)(2,1)} %param.11) | copy-start | bytes 3145732
  1.5 4.9 %copy-start.1 = (bf16[2,512,4,128]{3,2,1,0:T(4,128)(2,1)S(1)}, bf16[2,512,4,128]{3,2,1,0:T(4,128)(2,1)}, u32[]{:S(2)}) copy-start(bf16[2,512,4,128]{3,2,1,0:T(4,128)(2,1)} %param.10) | copy-start | bytes 3145732
  108.6 5.1 %collective-permute-start = (bf16[16,3,1024]{2,0,1:T(8,128)(2,1)S(1)}, bf16[16,3,1024]{2,0,1:T(8,128)(2,1)S(1)}, u32[]{:S(2)}, u32[]{:S(2)}) collective-permute-start(bf16[16,3,1024]{2,0,1:T(8,128)(2,1)S(1)} %dynamic-slice_bitcast_fusion), channel_id=1, source_target_pairs={{0,1},{1,0},{2,3},{3,2},{4,5},{5,4},{6,7},{7,6},{8,9},{9,8},{10,11... | collective-permute-start | bytes 294920 | tf_op jit(solution)/shard_map/ppermute | solution.py:373

commit v2 on v1

--- a/solution.py
+++ b/solution.py
@@ -194,7 +194,7 @@
         suf_st[head, 1] = jnp.concatenate(sums, axis=0)
         return carry
 
-    lax.fori_loop(0, kv, suffix, 0)
+    lax.fori_loop(0, kv, suffix, 0, unroll=True)
 
     def prefix(unit):
         chip = 2 * unit
@@ -213,7 +213,7 @@
                 stats[unit, i % 2, pl.ds(2 * head + 1, 1), :] = to_lanes(total[block])
             return carry
 
-        lax.fori_loop(0, kv, one, 0)
+        lax.fori_loop(0, kv, one, 0, unroll=True)
         return (
             send(psend.at[unit], precv.at[unit], ps_sem.at[unit], pr_sem.at[unit], 1),
             send(
@@ -246,7 +246,7 @@
                 ).astype(BF16)
                 return carry
 
-            lax.fori_loop(0, kv, one, 0)
+            lax.fori_loop(0, kv, one, 0, unroll=True)
             if chip:
                 outgoing.append(
                     send(csend.at[chip], crecv.at[chip], cs_sem.at[chip], cr_sem.at[chip], 2 * chip)
@@ -290,7 +290,7 @@
         att[0, head] = (mixed / total).astype(BF16)
         return carry
 
-    lax.fori_loop(0, kv, merge, 0)
+    lax.fori_loop(0, kv, merge, 0, unroll=True)
     attention = Gather(att, att.at[0], as_sem, ar_sem)
     attention.begin()
     attention.near()
@@ -365,7 +365,8 @@
         .reshape(n * forks * steps, heads * hd)
     )
     product = jnp.dot(attention, out_weight, preferred_element_type=F32)
-    product = product.reshape(tp, n * forks // tp, steps, -1).astype(BF16)
+    product = lax.optimization_barrier(product.astype(BF16))
+    product = product.reshape(tp, n * forks // tp, steps, -1)
     mine = lax.axis_index("tp")
     total = lax.dynamic_index_in_dim(product, mine, 0, keepdims=False).astype(F32)
     for shift in range(1, tp):

time: 115 us -> 101 us (0.88)
  Pallas kernels: 84.2 us -> 74.9 us
  local copies, waits for them, and re-layouts: 15.1 us -> 11.7 us
    pallas_call x1, Pallas kernels: 84.2 us -> 74.9 us  [shards(): pl.pallas_call(functools.partial(attend, n, steps), out_shape=jax.ShapeDt...]
    dot_general x1 -> x0, local copies, waits for them, and re-layouts: 3.97 us -> none  [shards(): product = jnp.dot(attention, out_weight, preferred_element_type=F32)]
    reshape x1, local copies, waits for them, and re-layouts: 3.01 us -> 1.84 us  [shards(): gathered.reshape(n, kv, forks * steps, group, hd).transpose(0, 2, 1, 3, 4)]
where the time goes in v2:
time: 101 us
  Pallas kernels  74.9 us (74%)
  local copies, waits for them, and re-layouts  11.7 us (12%)
  matrix products  8.54 us (8%)
  waiting for transfers between devices  4.27 us (4%)
  starting transfers between devices  1.57 us (2%)
    pallas_call x1, Pallas kernels, shards(): pl.pallas_call(functools.partial(attend, n, steps), out_shape=jax.ShapeDt...  74.9 us
    dot_general x1, matrix products, shards(): product = jnp.dot(attention, out_weight, preferred_element_type=F32)  8.54 us
    transpose x1, local copies, waits for them, and re-layouts, shards(): prefix_values.swapaxes(0, 1)  4.85 us
    ppermute x1, waiting for transfers between devices, shards(): lax.ppermute(piece, 'tp', [(i, (i + shift) % tp) for i in range(tp)])  4.27 us
  transfers between devices with their start and end apart: 1, of which 1 were waited for; matrix products, arithmetic and copies ran while one was open for 0% of the time, Pallas kernels for 0%

profile of v2, /device:TPU:0, one launch (start us, length us, event | category | flops | bytes accessed | tf_op | source)
XLA Modules:
  0.0 101.1 jit_solution(5255806895054056823)
XLA Ops:
  0.0 1.5 %copy.15 = bf16[6,4,16,128]{3,2,0,1:T(8,128)(2,1)} copy(bf16[6,4,16,128]{3,2,1,0:T(8,128)(2,1)} %bitcast.28) | data formatting | bytes 196608 | tf_op jit(solution)/shard_map/reshape | solution.py:313
  1.5 0.0 copy-start
  1.5 0.0 copy-start.1
  1.5 4.8 %copy_bitcast_fusion = (bf16[4,2048,128]{2,1,0:T(8,128)(2,1)}, bf16[4,2048,128]{2,1,0:T(8,128)(2,1)}) fusion(bf16[2048,4,128]{2,1,0:T(4,128)(2,1)} %param.9, bf16[2048,4,128]{2,1,0:T(4,128)(2,1)} %param.8), kind=kLoop, calls=%fused_computation | loop fusion | bytes 8388608 | tf_op jit(solution)/shard_map/transpose | solution.py:358
  6.4 0.0 copy-done
  6.4 0.0 copy-done.1
  6.4 1.7 %copy_bitcast_fusion.3 = (bf16[2,4,512,128]{3,2,1,0:T(8,128)(2,1)}, bf16[2,4,512,128]{3,2,1,0:T(8,128)(2,1)}) fusion(bf16[2,512,4,128]{3,2,1,0:T(4,128)(2,1)S(1)} %copy-done, bf16[2,512,4,128]{3,2,1,0:T(4,128)(2,1)S(1)} %copy-done.1), kind=kLoop, calls=%fused_computation.4 | loop fusion | bytes 4194304 | tf_op jit(solution)/shard_map/transpose | solution.py:360
  8.1 74.9 %shard_map.73 = bf16[16,4,96,128]{3,2,1,0:T(8,128)(2,1)} custom-call(s32[2]{0:T(128)} %lengths_ref.1, bf16[4,96,128]{2,1,0:T(8,128)(2,1)} %bitcast.27, bf16[4,2048,128]{2,1,0:T(8,128)(2,1)} %get-tuple-element.6.k_ref, bf16[4,2048,128]{2,1,0:T(8,128)(2,1)} %get-tuple-element.5.v_ref, bf16[2,4,512,128]{3,2,1,0:T(8,128)(2,1)} %get-tuple-element.8.sk_ref, ...), custom_call_target="tpu_custom_call" | custom-call | tf_op jit(solution)/shard_map/pallas_call | solution.py:318
  83.0 1.8 %copy.27 = bf16[16,4,6,16,128]{4,3,1,2,0:T(8,128)(2,1)S(1)} copy(bf16[16,4,6,16,128]{4,3,2,1,0:T(8,128)(2,1)} %bitcast.26) | data formatting | bytes 3145728 | tf_op jit(solution)/shard_map/reshape | solution.py:363
  84.8 0.9 reshape.20
  85.8 8.5 %convolution_convert_fusion = bf16[96,1024]{1,0:T(8,128)(2,1)S(1)} fusion(bf16[96,8192]{1,0:T(8,128)(2,1)S(1)} %reshape.20, bf16[8192,1024]{1,0:T(8,128)(2,1)} %param.13), kind=kOutput, calls=%fused_computation.3 | convolution fusion | flops 1610711040 | bytes 18546688 | tf_op jit(solution)/shard_map/dot_general | solution.py:367
  94.3 0.1 reshape.21
  94.5 0.1 dynamic-slice_bitcast_fusion
  94.5 1.6 %collective-permute-start = (bf16[16,3,1024]{2,1,0:T(4,128)(2,1)S(1)}, bf16[16,3,1024]{2,1,0:T(4,128)(2,1)S(1)}, u32[]{:S(2)}, u32[]{:S(2)}) collective-permute-start(bf16[16,3,1024]{2,1,0:T(4,128)(2,1)S(1)} %dynamic-slice_bitcast_fusion), channel_id=1, source_target_pairs={{0,1},{1,0},{2,3},{3,2},{4,5},{5,4},{6,7},{7,6},{8,9},{9,8},{10,11... | collective-permute-start | bytes 294920 | tf_op jit(solution)/shard_map/ppermute | solution.py:374
  96.1 4.3 %collective-permute-done = bf16[16,3,1024]{2,1,0:T(4,128)(2,1)S(1)} collective-permute-done((bf16[16,3,1024]{2,1,0:T(4,128)(2,1)S(1)}, bf16[16,3,1024]{2,1,0:T(4,128)(2,1)S(1)}, u32[]{:S(2)}, u32[]{:S(2)}) %collective-permute-start) | collective-permute-done | bytes 98336 | tf_op jit(solution)/shard_map/ppermute | solution.py:374
  100.4 0.1 fusion
  100.5 0.7 copy.21
Async XLA Ops:
  1.5 4.9 %copy-start = (bf16[2,512,4,128]{3,2,1,0:T(4,128)(2,1)S(1)}, bf16[2,512,4,128]{3,2,1,0:T(4,128)(2,1)}, u32[]{:S(2)}) copy-start(bf16[2,512,4,128]{3,2,1,0:T(4,128)(2,1)} %param.11) | copy-start | bytes 3145732
  1.5 4.9 %copy-start.1 = (bf16[2,512,4,128]{3,2,1,0:T(4,128)(2,1)S(1)}, bf16[2,512,4,128]{3,2,1,0:T(4,128)(2,1)}, u32[]{:S(2)}) copy-start(bf16[2,512,4,128]{3,2,1,0:T(4,128)(2,1)} %param.10) | copy-start | bytes 3145732
  94.5 5.8 %collective-permute-start = (bf16[16,3,1024]{2,1,0:T(4,128)(2,1)S(1)}, bf16[16,3,1024]{2,1,0:T(4,128)(2,1)S(1)}, u32[]{:S(2)}, u32[]{:S(2)}) collective-permute-start(bf16[16,3,1024]{2,1,0:T(4,128)(2,1)S(1)} %dynamic-slice_bitcast_fusion), channel_id=1, source_target_pairs={{0,1},{1,0},{2,3},{3,2},{4,5},{5,4},{6,7},{7,6},{8,9},{9,8},{10,11... | collective-permute-start | bytes 294920 | tf_op jit(solution)/shard_map/ppermute | solution.py:374
